TPU v7x, 512 devices: a 4x2x32 block of a 4x8x32 slice. The times are simulated.
512 devices in a mesh: groups: 2 (over y), seq: 32 (over z), sample: 4 (over x), vocab: 2 (over core).
Axes of the slice: x: 4, y: 2, z: 32, core: 2. Of those that a mesh axis runs over, the one named last changes fastest.
The devices are a block of a 4x8x32 slice.
Arguments:
- queries: bfloat16 [16, 2048, 1792], P(('groups', 'sample'), 'seq', 'vocab'), parts along dimension 0, may hold values from -130 to 130
- key_states: bfloat16 [16, 2048, 256], P(('groups', 'sample'), 'seq', 'vocab'), parts along dimension 0, may hold values from -8 to 8
- value_states: bfloat16 [16, 2048, 256], P(('groups', 'sample'), 'seq', 'vocab'), parts along dimension 0, may hold values from -6 to 6
- residual: bfloat16 [16, 2048, 1792], P(('groups', 'sample'), 'seq'), parts along dimension 0, may hold values from -3 to 3
- out_weight: bfloat16 [1792, 1792], P('vocab'), may hold values from -0.5 to 0.5
- norm_gain: float32 [1792], replicated, may hold values from 0.5 to 1.5
- vocab_head: bfloat16 [81920, 1792], P(('seq', 'sample', 'vocab')), may hold values from -21 to 21
- targets: int32 [16, 2048], P(('groups', 'sample')), parts along dimension 0, may hold values from 0 to 81919
- scored_slots: int32 [16, 512], P(('groups', 'sample')), parts along dimension 0, may hold values from -1 to 2047, as said below
- lengths: int32 [16], P(('groups', 'sample')), parts along dimension 0, may hold values from 512 to 2048
- rewards: int32 [16], P(('groups', 'sample')), parts along dimension 0, may hold values from 0 to 4
Outputs:
- token_logprobs: float32 [16, 512], P(('groups', 'sample'), 'seq'), parts along dimension 0
- seq_scores: float32 [16], P(('groups', 'sample')), parts along dimension 0
- advantages: float32 [16], P(('groups', 'sample')), parts along dimension 0
- objective: float32 [2], P('groups'), parts along dimension 0
There are 2 independent parts, one for each index of `groups`. A program takes and returns all parts, laid end to end along the dimension named above; an argument that names none is the same for every part. Nothing has to cross between parts.
Inputs may be any that keep to these rules, and one draw needn't show every extreme that they name: `scored_slots`: slots b * 16 to (b + 1) * 16 - 1 of a completion hold distinct positions of b * 64 to (b + 1) * 64 - 1 in rising order, followed by -1 in unused slots; every completion fills all 16 slots of some block; positions not listed are not scored. Positions from lengths[i] on are padding.
All inputs are finite; a program needn't handle non-finite values.
Results may differ from a plain program's by a relative error of at most 0.0085.
Values may be sent and summed in bfloat16 or wider, within the bound.
A program may use at most 64 MiB of HBM per device.

v0:
```python
import jax
import jax.numpy as jnp
from jax import lax
from jax.sharding import PartitionSpec as P

HD = 128
K = 8
floor_value = -1e30


def side_by_side(arrays, axis, dim, along):
    both = jnp.concatenate(arrays, axis=along)
    whole, at, gathered = (lax.all_gather(both, axis, axis=dim, tiled=True), 0, [])
    for a in arrays:
        gathered.append(lax.slice_in_dim(whole, at, at + a.shape[along], axis=along))
        at += a.shape[along]
    return tuple(gathered)


def sent_to_all(value, axis):
    copies = jnp.broadcast_to(value, (lax.axis_size(axis), *value.shape))
    return lax.all_to_all(copies, axis, split_axis=0, concat_axis=0, tiled=True)


def taken_together(value, axis):
    return sent_to_all(value, axis).astype(jnp.float32).sum(axis=0)


def all_in_one(value, axis):
    leaves = jax.tree.leaves(value)
    turns = sorted(range(len(leaves)), key=lambda k: -leaves[k].size)
    width = (1, *leaves[turns[0]].shape)[-1]
    lines = [
        jnp.pad(leaves[k].reshape(-1), (0, -leaves[k].size % width)).reshape(-1, width)
        for k in turns
    ]
    both, at, found = (lax.all_gather(jnp.concatenate(lines), axis), 0, {})
    for k, line in zip(turns, lines):
        slab = both[:, at : at + len(line)].reshape(len(both), -1)
        found[k] = slab[:, : leaves[k].size].reshape(-1, *leaves[k].shape)
        at += len(line)
    numbers = iter(range(len(leaves)))
    return jax.tree.map(lambda _: found[next(numbers)], value)


def joined(value, axis, combine):
    everything = all_in_one(value, axis)
    initial = jax.tree.map(lambda part: part[0], everything)

    def turn(k, so_far):
        return combine(so_far, jax.tree.map(lambda part: part[k], everything))

    return lax.fori_loop(1, lax.axis_size(axis), turn, initial)


def rms_scale(hidden, norm_gain):
    power = jnp.mean(hidden * hidden, axis=-1, keepdims=True)
    return (hidden * lax.rsqrt(power + 1e-06) * norm_gain).astype(jnp.bfloat16)


def merge_stats(left, right):
    top_score = jnp.maximum(left[0], right[0])
    weight_sum = left[1] * jnp.exp(left[0] - top_score) + right[1] * jnp.exp(right[0] - top_score)
    return (top_score, weight_sum, left[2] + right[2])


def shards(
    queries,
    key_states,
    value_states,
    residual,
    out_weight,
    norm_gain,
    vocab_head,
    targets,
    scored_slots,
    lengths,
    rewards,
):
    sample_count, block_len, query_width = queries.shape
    kv_heads = key_states.shape[2] // HD
    group_size = query_width // HD // kv_heads
    model_width = out_weight.shape[1]
    full_len = targets.shape[1]
    slot_total = scored_slots.shape[1]
    slot_cap = slot_total // lax.axis_size("seq")
    first_pos = lax.axis_index("seq") * block_len
    query_pos = first_pos + jnp.arange(block_len, dtype=jnp.int32)
    query_view = queries.reshape(sample_count, block_len, kv_heads, group_size, HD)
    stat_shape = (sample_count, block_len, kv_heads, group_size)
    pieces = side_by_side((key_states, value_states), "seq", 1, 0)
    top_score = jnp.full(stat_shape, floor_value, jnp.float32)
    piece_len = pieces[0].shape[1]
    key_view = pieces[0].reshape(sample_count, piece_len, kv_heads, HD)
    value_view = pieces[1].reshape(sample_count, piece_len, kv_heads, HD)
    scores = jnp.einsum(
        "srkgd,snkd->srkgn", query_view, key_view, preferred_element_type=jnp.float32
    ) * HD ** (-0.5)
    key_pos = jnp.arange(piece_len, dtype=jnp.int32)
    allowed = (key_pos[None, :] <= query_pos[:, None])[None, :, None, None, :]
    masked = jnp.where(allowed, scores, floor_value)
    new_top = jnp.maximum(top_score, jnp.max(masked, axis=-1))
    weights = jnp.where(allowed, jnp.exp(masked - new_top[..., None]), 0.0)
    weight_sum = jnp.sum(weights, axis=-1)
    update = jnp.einsum(
        "srkgn,snkd->srkgd",
        weights.astype(jnp.bfloat16),
        value_view,
        preferred_element_type=jnp.float32,
    )
    weighted = update
    new_top, weight_sum, weighted = (new_top, weight_sum, weighted)
    safe_sum = jnp.where(weight_sum > 0, weight_sum, 1.0)
    attended = (
        (weighted / safe_sum[..., None])
        .reshape(sample_count, block_len, query_width)
        .astype(jnp.bfloat16)
    )
    own_slots = lax.dynamic_slice_in_dim(
        scored_slots, lax.axis_index("seq") * slot_cap, slot_cap, 1
    )
    local_pos = jnp.clip(own_slots - first_pos, 0, block_len - 1)
    picked_attended = jnp.take_along_axis(attended, local_pos[:, :, None], axis=1)
    picked_resid = jnp.take_along_axis(residual, local_pos[:, :, None], axis=1)
    partial_value = jnp.einsum(
        "scq,qd->scd", picked_attended, out_weight, preferred_element_type=jnp.float32
    )
    head_rows = lax.all_gather(vocab_head, "sample", axis=0, tiled=True)
    shard_rows = vocab_head.shape[0]
    row_index = jnp.arange(head_rows.shape[0], dtype=jnp.int32)
    owner = (
        lax.axis_index("seq") * lax.axis_size("sample") + row_index // shard_rows
    ) * lax.axis_size("vocab") + lax.axis_index("vocab")
    vocab_ids = owner * shard_rows + row_index % shard_rows
    summed = taken_together(partial_value.astype(jnp.bfloat16), "vocab").astype(jnp.float32)
    normed = rms_scale(picked_resid.astype(jnp.float32) + summed, norm_gain)
    pieces = lax.all_gather(normed, "seq", axis=1, tiled=True)
    piece_len = pieces.shape[1]
    flat = pieces.reshape(sample_count * piece_len, model_width)
    logits = lax.dot_general(
        flat, head_rows, (((1,), (1,)), ((), ())), preferred_element_type=jnp.float32
    )
    logits = logits.reshape(sample_count, piece_len, head_rows.shape[0])
    top_local = jnp.max(logits, axis=-1)
    sum_local = jnp.sum(jnp.exp(logits - top_local[..., None]), axis=-1)
    slot_piece = jnp.maximum(scored_slots, 0)
    wanted = jnp.take_along_axis(targets, slot_piece, axis=1)
    picked = jnp.sum(jnp.where(vocab_ids[None, None, :] == wanted[..., None], logits, 0.0), axis=-1)
    top_local, sum_local, pick_local = (top_local, sum_local, picked)
    top_all, sum_all, pick_all = joined(
        (top_local, sum_local, pick_local), ("seq", "vocab"), merge_stats
    )
    logprob = pick_all - (top_all + jnp.log(sum_all))
    scored = (scored_slots >= 0) & (scored_slots < lengths[:, None])
    token_all = jnp.where(scored, logprob, 0.0)
    own_scores = jnp.sum(token_all, axis=-1) / full_len
    own_tokens = lax.dynamic_slice_in_dim(token_all, lax.axis_index("seq") * slot_cap, slot_cap, 1)
    own_reward = rewards.astype(jnp.float32)
    reward_all, score_all = (
        lax.all_gather(own_reward, "sample", axis=0, tiled=True),
        lax.all_gather(own_scores, "sample", axis=0, tiled=True),
    )
    reward_sum = jnp.sum(reward_all)
    own_advantage = own_reward - (reward_sum - own_reward) / (K - 1)
    every_advantage = reward_all - (reward_sum - reward_all) / (K - 1)
    objective = -(jnp.sum(every_advantage * score_all) / K).reshape(1)
    return (own_tokens, own_scores, own_advantage, objective)


def solution(mesh):
    in_specs = (
        P(("groups", "sample"), "seq", "vocab"),
        P(("groups", "sample"), "seq", "vocab"),
        P(("groups", "sample"), "seq", "vocab"),
        P(("groups", "sample"), "seq", None),
        P("vocab", None),
        P(),
        P(("seq", "sample", "vocab"), None),
        P(("groups", "sample"), None),
        P(("groups", "sample"), None),
        P(("groups", "sample")),
        P(("groups", "sample")),
    )
    out_specs = (
        P(("groups", "sample"), "seq"),
        P(("groups", "sample")),
        P(("groups", "sample")),
        P("groups"),
    )
    return jax.shard_map(shards, mesh=mesh, in_specs=in_specs, out_specs=out_specs, check_vma=False)
```

profile of v0, /device:TPU:40, one launch (start us, length us, event | category | flops | bytes accessed | tf_op | source)
XLA Modules:
  0.0 512.0 jit_solution(15304321632450815917)
XLA Ops:
  7.3 1.5 pad_maximum_fusion
  8.9 0.7 all-gather.10.cloned.1.call-update
  9.8 0.8 compare_and_fusion
  10.6 2.6 gather_fusion
  13.4 157.4 %all-gather.6.cloned.1.call-done = bf16[4,2048,128]{2,1,0:T(8,128)(2,1)} async-done(((bf16[4,64,128]{2,1,0:T(8,128)(2,1)}), bf16[4,2048,128]{2,1,0:T(8,128)(2,1)}) %all-gather.6.cloned.1.call-update) | async-done | bytes 2097168 | tf_op jit(solution)/shard_map/all_gather | solution.py:13
  170.8 2.7 fusion.2
  173.5 2.2 fusion.3
  175.7 1.6 fusion.26
  177.3 0.9 copy.21
  178.2 1.2 convert_element_type.31
  179.4 0.8 gather_fusion.1
  180.9 3.9 all_to_all.5
  185.1 0.8 multiply_convert_fusion
  186.0 9.1 %gather_fusion.2 = s32[1024]{0:T(1024)S(1)} fusion(s32[2,2048]{1,0:T(2,128)S(1)} %copy-done.1, s32[1024]{0:T(1024)S(1)} %bitcast.125), kind=kCustom, calls=%fused_computation.2 | custom fusion | bytes 16384 | tf_op jit(solution)/shard_map/jit(take_along_axis)/gather | solution.py:147
  195.1 1.3 dynamic-slice
  197.2 34.9 %all-gather.10.cloned.1.call-done = bf16[1280,1792]{1,0:T(8,128)(2,1)} async-done(((bf16[320,1792]{1,0:T(8,128)(2,1)}), bf16[1280,1792]{1,0:T(8,128)(2,1)}) %all-gather.10.cloned.1.call-update) | async-done | bytes 4587536 | tf_op jit(solution)/shard_map/all_gather | solution.py:128
  232.1 142.7 %all-gather.8.cloned.1.call-done = bf16[2,512,1792]{2,1,0:T(8,128)(2,1)} async-done(((bf16[2,16,1792]{2,1,0:T(8,128)(2,1)}), bf16[2,512,1792]{2,1,0:T(8,128)(2,1)}) %all-gather.8.cloned.1.call-update) | async-done | bytes 3670032 | tf_op jit(solution)/shard_map/all_gather | solution.py:137
  374.7 8.5 %fusion.54 = (f32[2,512]{1,0:T(2,128)S(1)}, f32[2,512,1280]{2,1,0:T(8,128)S(1)}) fusion(bf16[2,512,1792]{2,1,0:T(8,128)(2,1)} %all-gather.8.cloned.1.call-done, bf16[1280,1792]{1,0:T(8,128)(2,1)} %all-gather.10.cloned.1.call-done), kind=kOutput, calls=%fused_computation.86 | convolution fusion | flops 4698930176 | bytes 13504512 | tf_op jit(solution)/shard_map/dot_general | solution.py:140
  383.2 1.5 exponential_reduce_fusion
  384.8 57.0 %all-gather.1 = f32[64,6,512]{2,1,0:T(8,128)S(1)} all-gather(f32[1,6,512]{2,1,0:T(8,128)S(1)} %maximum_bitcast_fusion), channel_id=2, replica_groups=mesh['groups'=2,'seq'=32,'sample'=4,'vocab'=2] {'seq','vocab'}, dimensions={0}, use_global_device_ids=true | all-gather | bytes 798720 | tf_op jit(solution)/shard_map/all_gather | solution.py:37
  441.7 1.1 fusion.53
  442.8 46.1 %while.19 = (s32[]{:T(128)}, f32[2,512]{1,0:T(2,128)S(1)}, f32[2,512]{1,0:T(2,128)S(1)}, f32[2,512]{1,0:T(2,128)S(1)}, f32[64,2,512]{2,1,0:T(2,128)}, /*index=5*...) while((s32[]{:T(128)}, f32[2,512]{1,0:T(2,128)S(1)}, ...), condition=%wide.region_8.9_spmd, body=%wide.region_7.8_spmd.sunk | while | flops 7173 | bytes 37011 | solution.py:53
  443.5 0.7 fusion.58
  444.2 0.7 fusion.58
  445.0 0.7 fusion.58
  446.4 0.7 fusion.58
  447.9 0.7 fusion.58
  448.6 0.7 fusion.58
  449.4 0.7 fusion.58
  452.3 0.7 fusion.58
  453.0 0.7 fusion.58
  453.7 0.7 fusion.58
  454.5 0.7 fusion.58
  455.2 0.8 fusion.58
  456.0 0.7 fusion.58
  456.7 0.7 fusion.58
  457.5 0.7 fusion.58
  458.2 0.7 fusion.58
  459.0 0.7 fusion.58
  459.7 0.7 fusion.58
  461.2 0.7 fusion.58
  461.9 0.7 fusion.58
  463.4 0.7 fusion.58
  466.3 0.7 fusion.58
  467.7 0.7 fusion.58
  468.4 0.7 fusion.58
  469.9 0.7 fusion.58
  471.4 0.7 fusion.58
  472.1 0.7 fusion.58
  473.5 0.7 fusion.58
  474.3 0.7 fusion.58
  475.7 0.7 fusion.58
  476.5 0.7 fusion.58
  477.2 0.7 fusion.58
  478.7 0.7 fusion.58
  479.4 0.7 fusion.58
  481.7 0.7 fusion.58
  483.1 0.7 fusion.58
  483.8 0.7 fusion.58
  487.5 0.7 fusion.58
  488.2 0.7 fusion.58
  489.7 10.3 %all-reduce.2 = (f32[8]{0:T(128)S(1)}, f32[8]{0:T(128)S(1)}) all-reduce(f32[8]{0:T(128)S(1)} %convert_dynamic-update-slice_fusion, f32[8]{0:T(128)S(1)} %get-tuple-element.205), channel_id=1, replica_groups=mesh['groups'=2,'seq'=32,'sample'=4,'vocab'=2] {'sample'}, use_global_device_ids=true, to_apply=%add | all-reduce | flops 16 | bytes 128
  500.6 1.2 multiply_subtract_fusion
  501.8 1.2 multiply_reduce_fusion.1
  (70 shorter events, 20.6 us)
Async XLA Ops:
  7.2 173.1 %copy-start = (bf16[896,1792]{1,0:T(8,128)(2,1)S(1)}, bf16[896,1792]{1,0:T(8,128)(2,1)}, u32[]{:S(2)}) copy-start(bf16[896,1792]{1,0:T(8,128)(2,1)} %param.17) | copy-start | bytes 9633796
  7.2 163.6 %all-gather.6.cloned.1.call-start = ((), (), s32[]{:S(2)}) async-start(), calls=%async_computation.1 | async-start | bytes 2162688 | tf_op jit(solution)/shard_map/all_gather | solution.py:13
  8.9 223.2 %all-gather.10.cloned.1.call-start = ((), (), s32[]{:S(2)}) async-start(), calls=%async_computation.3 | async-start | bytes 5734400 | tf_op jit(solution)/shard_map/all_gather | solution.py:128
  9.7 365.0 %all-gather.8.cloned.1.call-start = ((), (), s32[]{:S(2)}) async-start(), calls=%async_computation.2 | async-start | bytes 3784704 | tf_op jit(solution)/shard_map/all_gather | solution.py:137
  173.5 2.3 copy-start.3
  177.3 7.8 %copy-start.5 = (f32[1792]{0:T(1024)S(1)}, f32[1792]{0:T(1024)}, u32[]{:S(2)}) copy-start(f32[1792]{0:T(1024)} %param.18) | copy-start | bytes 21508
  177.3 8.6 %copy-start.4 = (s32[2,512]{1,0:T(2,128)S(1)}, s32[2,512]{1,0:T(2,128)}, u32[]{:S(2)}) copy-start(s32[2,512]{1,0:T(2,128)} %param.21) | copy-start | bytes 12292
  177.3 8.6 %copy-start.1 = (s32[2,2048]{1,0:T(2,128)S(1)}, s32[2,2048]{1,0:T(2,128)}, u32[]{:S(2)}) copy-start(s32[2,2048]{1,0:T(2,128)} %param.20) | copy-start | bytes 49156
  180.3 4.6 copy-start.2
  180.3 16.8 %copy-start.7 = (s32[2]{0:T(128)S(1)}, s32[2]{0:T(128)}, u32[]{:S(2)}) copy-start(s32[2]{0:T(128)} %param.23) | copy-start | bytes 28
  383.2 105.7 %copy-start.6 = (s32[2]{0:T(128)S(1)}, s32[2]{0:T(128)}, u32[]{:S(2)}) copy-start(s32[2]{0:T(128)} %param.22) | copy-start | bytes 28
Sparse Core Ops, SparseCore 0:
  10.1 160.6 all-gather.5
  172.9 59.0 all-gather.9
  234.2 140.4 all-gather.7
where the time goes:
time: 517 us; the launch traced here: 512 us
  waiting for transfers between devices  336 us (65%)
  blocking collectives  71.2 us (14%)
  other arithmetic  56.3 us (11%)
  local copies, waits for them, and re-layouts  17.8 us (3%)
  between operations  16.5 us (3%)
  matrix products  13.3 us (3%)
    all_gather x1, waiting for transfers between devices, side_by_side(): lax.all_gather(both, axis, axis=dim, tiled=True)  157 us
    all_gather x1, waiting for transfers between devices, shards(): pieces = lax.all_gather(normed, 'seq', axis=1, tiled=True)  143 us
    all_gather x1, blocking collectives, all_in_one(): both, at, found = (lax.all_gather(jnp.concatenate(lines), axis), 0, {})  57 us
    add x63, other arithmetic, merge_stats(): left[1] * jnp.exp(left[0] - top_score)  45.2 us
    all_gather x1, waiting for transfers between devices, shards(): head_rows = lax.all_gather(vocab_head, 'sample', axis=0, tiled=True)  34.9 us
  transfers between devices with their start and end apart: 3, of which 3 were waited for; matrix products, arithmetic and copies ran while one was open for 5% of the time, Pallas kernels for 0%

commit v1 on v0

--- a/solution.py
+++ b/solution.py
@@ -6,6 +6,19 @@
 HD = 128
 K = 8
 floor_value = -1e30
+
+
+def collect(x, axis, dim):
+    size, mine, rows = (lax.axis_size(axis), lax.axis_index(axis), x.shape[dim])
+    upward = [(i, (i + 1) % size) for i in range(size)]
+    filled = jnp.zeros((*x.shape[:dim], size * rows, *x.shape[dim + 1 :]), x.dtype)
+    block = x
+    for step in range(size):
+        owner = (mine - step) % size
+        filled = lax.dynamic_update_slice_in_dim(filled, block, owner * rows, axis=dim)
+        if step < size - 1:
+            block = lax.ppermute(block, axis, upward)
+    return filled
 
 
 def side_by_side(arrays, axis, dim, along):
@@ -125,7 +138,7 @@
     partial_value = jnp.einsum(
         "scq,qd->scd", picked_attended, out_weight, preferred_element_type=jnp.float32
     )
-    head_rows = lax.all_gather(vocab_head, "sample", axis=0, tiled=True)
+    head_rows = collect(vocab_head, "sample", 0)
     shard_rows = vocab_head.shape[0]
     row_index = jnp.arange(head_rows.shape[0], dtype=jnp.int32)
     owner = (

time: 517 us -> 460 us (0.89)
  waiting for transfers between devices: 336 us -> 260 us
  local copies, waits for them, and re-layouts: 17.8 us -> 28.3 us
  starting transfers between devices: 0.19 us -> 8.1 us
    all_gather x1, waiting for transfers between devices: 143 us -> 39.3 us  [shards(): pieces = lax.all_gather(normed, 'seq', axis=1, tiled=True)]
    ppermute x0 -> x3, waiting for transfers between devices: none -> 62.2 us  [collect(): block = lax.ppermute(block, axis, upward)]
    all_gather x1 -> x0, waiting for transfers between devices: 34.9 us -> none  [shards(): head_rows = lax.all_gather(vocab_head, 'sample', axis=0, tiled=True)]
    dynamic_update_slice x0 -> x4, local copies, waits for them, and re-layouts: none -> 8.15 us  [collect(): lax.dynamic_update_slice_in_dim(filled, block, owner * rows, axis=dim)]
    ppermute x0 -> x3, starting transfers between devices: none -> 7.97 us  [collect(): block = lax.ppermute(block, axis, upward)]
  transfers between devices with their start and end apart: 3 -> 5, of which waited for: 3 -> 5; matrix products, arithmetic and copies ran while one was open for 5% -> 5% of each run, Pallas kernels for 0% -> 0%
where the time goes in v1:
time: 460 us; the launch traced here: 455 us
  waiting for transfers between devices  260 us (57%)
  blocking collectives  70.9 us (15%)
  other arithmetic  56.5 us (12%)
  local copies, waits for them, and re-layouts  28.3 us (6%)
  between operations  16.9 us (4%)
  matrix products  13.3 us (3%)
  starting transfers between devices  8.1 us (2%)
    all_gather x1, waiting for transfers between devices, side_by_side(): lax.all_gather(both, axis, axis=dim, tiled=True)  158 us
    ppermute x3, waiting for transfers between devices, collect(): block = lax.ppermute(block, axis, upward)  62.2 us
    all_gather x1, blocking collectives, all_in_one(): both, at, found = (lax.all_gather(jnp.concatenate(lines), axis), 0, {})  56.3 us
    add x63, other arithmetic, merge_stats(): left[1] * jnp.exp(left[0] - top_score)  45.2 us
    all_gather x1, waiting for transfers between devices, shards(): pieces = lax.all_gather(normed, 'seq', axis=1, tiled=True)  39.3 us
    unnamed x1, blocking collectives  10.6 us
  transfers between devices with their start and end apart: 5, of which 5 were waited for; matrix products, arithmetic and copies ran while one was open for 5% of the time, Pallas kernels for 0%

profile of v1, /device:TPU:40, one launch (start us, length us, event | category | flops | bytes accessed | tf_op | source)
XLA Modules:
  0.0 454.8 jit_solution(3630867505777340210)
XLA Ops:
  7.3 1.6 pad_maximum_fusion
  9.0 0.8 compare_and_fusion
  9.8 2.6 gather_fusion
  12.6 158.2 %all-gather.5.cloned.1.call-done = bf16[4,2048,128]{2,1,0:T(8,128)(2,1)} async-done(((bf16[4,64,128]{2,1,0:T(8,128)(2,1)}), bf16[4,2048,128]{2,1,0:T(8,128)(2,1)}) %all-gather.5.cloned.1.call-update) | async-done | bytes 2097168 | tf_op jit(solution)/shard_map/all_gather | solution.py:26
  170.8 2.6 fusion.2
  173.5 2.2 fusion.3
  175.7 1.6 fusion.26
  177.3 0.8 copy.21
  178.2 1.2 convert_element_type.31
  179.4 0.8 gather_fusion.1
  180.9 3.9 all_to_all.5
  185.0 0.8 multiply_convert_fusion
  185.9 3.7 collective-permute-start
  189.5 27.2 %collective-permute-done = bf16[320,1792]{1,0:T(8,128)(2,1)} collective-permute-done((bf16[320,1792]{1,0:T(8,128)(2,1)}, bf16[320,1792]{1,0:T(8,128)(2,1)}, u32[]{:S(2)}, u32[]{:S(2)}) %collective-permute-start) | collective-permute-done | bytes 1146912 | tf_op jit(solution)/shard_map/ppermute | solution.py:20
  216.7 2.4 collective-permute-start.1
  219.1 1.3 dynamic-slice
  221.0 25.6 %collective-permute-done.1 = bf16[320,1792]{1,0:T(8,128)(2,1)} collective-permute-done((bf16[320,1792]{1,0:T(8,128)(2,1)}, bf16[320,1792]{1,0:T(8,128)(2,1)}, u32[]{:S(2)}, u32[]{:S(2)}) %collective-permute-start.1) | collective-permute-done | bytes 1146912 | tf_op jit(solution)/shard_map/ppermute | solution.py:20
  246.6 1.9 collective-permute-start.2
  248.9 9.1 %gather_fusion.2 = s32[1024]{0:T(1024)S(1)} fusion(s32[2,2048]{1,0:T(2,128)S(1)} %copy-done.1, s32[1024]{0:T(1024)S(1)} %bitcast.125), kind=kCustom, calls=%fused_computation.2 | custom fusion | bytes 16384 | tf_op jit(solution)/shard_map/jit(take_along_axis)/gather | solution.py:160
  258.1 2.4 broadcast_in_dim.82
  260.5 1.1 constant_dynamic-update-slice_fusion.3
  261.6 2.4 constant_dynamic-update-slice_fusion.2
  263.9 2.3 constant_dynamic-update-slice_fusion.1
  266.3 9.5 %collective-permute-done.2 = bf16[320,1792]{1,0:T(8,128)(2,1)} collective-permute-done((bf16[320,1792]{1,0:T(8,128)(2,1)}, bf16[320,1792]{1,0:T(8,128)(2,1)}, u32[]{:S(2)}, u32[]{:S(2)}) %collective-permute-start.2) | collective-permute-done | bytes 1146912 | tf_op jit(solution)/shard_map/ppermute | solution.py:20
  275.7 2.4 constant_dynamic-update-slice_fusion
  278.1 39.3 %all-gather.7.cloned.1.call-done = bf16[2,512,1792]{2,1,0:T(8,128)(2,1)} async-done(((bf16[2,16,1792]{2,1,0:T(8,128)(2,1)}), bf16[2,512,1792]{2,1,0:T(8,128)(2,1)}) %all-gather.7.cloned.1.call-update) | async-done | bytes 3670032 | tf_op jit(solution)/shard_map/all_gather | solution.py:150
  317.4 8.5 %fusion.56 = (f32[2,512]{1,0:T(2,128)S(1)}, f32[2,512,1280]{2,1,0:T(8,128)S(1)}) fusion(bf16[2,512,1792]{2,1,0:T(8,128)(2,1)} %all-gather.7.cloned.1.call-done, bf16[1280,1792]{1,0:T(8,128)(2,1)} %constant_dynamic-update-slice_fusion), kind=kOutput, calls=%fused_computation.93 | convolution fusion | flops 4698930176 | bytes 13504512 | tf_op jit(solution)/shard_map/dot_general | solution.py:153
  325.9 1.5 exponential_reduce_fusion
  327.5 56.3 %all-gather.1 = f32[64,6,512]{2,1,0:T(8,128)S(1)} all-gather(f32[1,6,512]{2,1,0:T(8,128)S(1)} %maximum_bitcast_fusion), channel_id=2, replica_groups=mesh['groups'=2,'seq'=32,'sample'=4,'vocab'=2] {'seq','vocab'}, dimensions={0}, use_global_device_ids=true | all-gather | bytes 798720 | tf_op jit(solution)/shard_map/all_gather | solution.py:50
  383.8 1.1 fusion.55
  384.9 46.1 %while.19 = (s32[]{:T(128)}, f32[2,512]{1,0:T(2,128)S(1)}, f32[2,512]{1,0:T(2,128)S(1)}, f32[2,512]{1,0:T(2,128)S(1)}, f32[64,2,512]{2,1,0:T(2,128)}, /*index=5*...) while((s32[]{:T(128)}, f32[2,512]{1,0:T(2,128)S(1)}, ...), condition=%wide.region_8.9_spmd, body=%wide.region_7.8_spmd.sunk | while | flops 7173 | bytes 37011 | solution.py:66
  385.6 0.7 fusion.60
  386.3 0.7 fusion.60
  387.1 0.7 fusion.60
  388.5 0.7 fusion.60
  390.0 0.7 fusion.60
  390.7 0.7 fusion.60
  391.4 0.7 fusion.60
  395.1 0.7 fusion.60
  395.8 0.7 fusion.60
  396.6 0.7 fusion.60
  397.3 0.8 fusion.60
  398.8 0.7 fusion.60
  399.6 0.7 fusion.60
  400.3 0.7 fusion.60
  401.1 0.7 fusion.60
  401.8 0.7 fusion.60
  403.3 0.7 fusion.60
  405.5 0.7 fusion.60
  408.4 0.7 fusion.60
  409.8 0.7 fusion.60
  410.5 0.7 fusion.60
  413.5 0.7 fusion.60
  415.6 0.7 fusion.60
  416.4 0.7 fusion.60
  417.8 0.7 fusion.60
  419.3 0.7 fusion.60
  420.8 0.7 fusion.60
  421.5 0.7 fusion.60
  423.7 0.7 fusion.60
  429.6 0.7 fusion.60
  432.4 10.6 %all-reduce.2 = (f32[8]{0:T(128)S(1)}, f32[8]{0:T(128)S(1)}) all-reduce(f32[8]{0:T(128)S(1)} %convert_dynamic-update-slice_fusion, f32[8]{0:T(128)S(1)} %get-tuple-element.205), channel_id=1, replica_groups=mesh['groups'=2,'seq'=32,'sample'=4,'vocab'=2] {'sample'}, use_global_device_ids=true, to_apply=%add | all-reduce | flops 16 | bytes 128
  443.6 1.2 multiply_subtract_fusion
  444.8 1.3 multiply_reduce_fusion.1
  (80 shorter events, 27.1 us)
Async XLA Ops:
  7.2 173.1 %copy-start = (bf16[896,1792]{1,0:T(8,128)(2,1)S(1)}, bf16[896,1792]{1,0:T(8,128)(2,1)}, u32[]{:S(2)}) copy-start(bf16[896,1792]{1,0:T(8,128)(2,1)} %param.17) | copy-start | bytes 9633796
  7.2 163.6 %all-gather.5.cloned.1.call-start = ((), (), s32[]{:S(2)}) async-start(), calls=%async_computation.1 | async-start | bytes 2162688 | tf_op jit(solution)/shard_map/all_gather | solution.py:26
  8.9 308.6 %all-gather.7.cloned.1.call-start = ((), (), s32[]{:S(2)}) async-start(), calls=%async_computation.2 | async-start | bytes 3784704 | tf_op jit(solution)/shard_map/all_gather | solution.py:150
  173.5 2.3 copy-start.4
  177.3 7.7 %copy-start.6 = (f32[1792]{0:T(1024)S(1)}, f32[1792]{0:T(1024)}, u32[]{:S(2)}) copy-start(f32[1792]{0:T(1024)} %param.18) | copy-start | bytes 21508
  177.3 43.7 %copy-start.5 = (s32[2,512]{1,0:T(2,128)S(1)}, s32[2,512]{1,0:T(2,128)}, u32[]{:S(2)}) copy-start(s32[2,512]{1,0:T(2,128)} %param.21) | copy-start | bytes 12292
  177.3 71.3 %copy-start.8 = (s32[2]{0:T(128)S(1)}, s32[2]{0:T(128)}, u32[]{:S(2)}) copy-start(s32[2]{0:T(128)} %param.23) | copy-start | bytes 28
  177.3 71.6 %copy-start.1 = (s32[2,2048]{1,0:T(2,128)S(1)}, s32[2,2048]{1,0:T(2,128)}, u32[]{:S(2)}) copy-start(s32[2,2048]{1,0:T(2,128)} %param.20) | copy-start | bytes 49156
  180.2 4.6 %copy-start.3 = (bf16[32,1792]{1,0:T(8,128)(2,1)S(1)}, bf16[32,1792]{1,0:T(8,128)(2,1)}, u32[]{:S(2)}) copy-start(bf16[32,1792]{1,0:T(8,128)(2,1)} %gather_fusion) | copy-start | bytes 344068
  185.9 30.8 %collective-permute-start = (bf16[320,1792]{1,0:T(8,128)(2,1)}, bf16[320,1792]{1,0:T(8,128)(2,1)}, u32[]{:S(2)}, u32[]{:S(2)}) collective-permute-start(bf16[320,1792]{1,0:T(8,128)(2,1)} %param.19), channel_id=1, source_target_pairs={{0,2},{2,4},{4,6},{6,0},{1,3},{3,5},{5,7},{7,1},{8,10},{10,12},{12... | collective-permute-start | bytes 3440648 | tf_op jit(solution)/shard_map/ppermute | solution.py:20
  216.7 29.9 %collective-permute-start.1 = (bf16[320,1792]{1,0:T(8,128)(2,1)}, bf16[320,1792]{1,0:T(8,128)(2,1)}, u32[]{:S(2)}, u32[]{:S(2)}) collective-permute-start(bf16[320,1792]{1,0:T(8,128)(2,1)} %collective-permute-done), channel_id=1, source_target_pairs={{0,2},{2,4},{4,6},{6,0},{1,3},{3,5},{5,7},{7,1},{8,10},{10,12},{12... | collective-permute-start | bytes 3440648 | tf_op jit(solution)/shard_map/ppermute | solution.py:20
  246.6 29.1 %collective-permute-start.2 = (bf16[320,1792]{1,0:T(8,128)(2,1)}, bf16[320,1792]{1,0:T(8,128)(2,1)}, u32[]{:S(2)}, u32[]{:S(2)}) collective-permute-start(bf16[320,1792]{1,0:T(8,128)(2,1)} %collective-permute-done.1), channel_id=1, source_target_pairs={{0,2},{2,4},{4,6},{6,0},{1,3},{3,5},{5,7},{7,1},{8,10},{10,12},{12... | collective-permute-start | bytes 3440648 | tf_op jit(solution)/shard_map/ppermute | solution.py:20
  258.1 2.4 copy-start.2
  325.9 105.1 %copy-start.7 = (s32[2]{0:T(128)S(1)}, s32[2]{0:T(128)}, u32[]{:S(2)}) copy-start(s32[2]{0:T(128)} %param.22) | copy-start | bytes 28
Sparse Core Ops, SparseCore 0:
  10.1 160.6 all-gather.4
  186.0 131.3 all-gather.6
